TPU v7x, 32 devices: a whole 2x2x4 slice. The times are simulated.
32 devices in a mesh: enc: 8 (over z, x), dec: 2 (over y), grp: 2 (over core).
Axes of the slice: x: 2, y: 2, z: 4, core: 2. Of those that a mesh axis runs over, the one named last changes fastest.
Arguments:
- images: bfloat16 [32, 4, 32, 1280], P(('enc', 'dec', 'grp')), may hold values from -6 to 6
- ln_gain: float32 [1280], replicated, may hold values from 0.1 to 1.9
- ln_bias: float32 [1280], replicated, may hold values from -3 to 3
- fc1_weight: bfloat16 [5120, 1280], P('enc'), may hold values from -0.15625 to 0.15625
- fc1_bias: float32 [5120], P('enc'), may hold values from -3 to 3
- fc2_weight: bfloat16 [5120, 1280], P('enc'), may hold values from -0.078125 to 0.078125
- fc2_bias: float32 [1280], replicated, may hold values from -3 to 3
- key_weight: bfloat16 [1280, 512], replicated, may hold values from -0.15625 to 0.15625
- value_weight: bfloat16 [1280, 512], replicated, may hold values from -0.15625 to 0.15625
- text: bfloat16 [32, 128, 8192], P(('enc', 'grp')), may hold values from -6 to 6
- query_weight: bfloat16 [8192, 4096], P('enc', 'dec'), may hold values from -0.0625 to 0.0625
- tiles: int32 [8, 2, 2], replicated, may hold values from 1 to 4, as said below
- links: int32 [32, 2], P(('enc', 'grp')), may hold values from 0 to 1, as said below
- lengths: int32 [32], P(('enc', 'grp')), may hold values from 1 to 128
- state_grads: bfloat16 [32, 4, 32, 1280], P(('enc', 'dec', 'grp')), may hold values from -0.125 to 0.125
Outputs:
- context: bfloat16 [32, 128, 4096], P(('enc', 'grp'), None, 'dec')
- fc1_grad: float32 [5120, 1280], P(('enc', 'dec', 'grp'))
- fc2_grad: float32 [5120, 1280], P(('enc', 'dec', 'grp'))
Inputs may be any that keep to these rules, and one draw needn't show every extreme that they name: The 8 images that share their last two indices have 20 tiles together, and one of them has 4. `links`: every text is linked to at least one image.
All inputs are finite; a program needn't handle non-finite values.
Results may differ from a plain program's by a relative error of at most 0.017.
Values may be sent and summed in bfloat16 or wider, within the bound.
A program may use at most 128 MiB of HBM per device.

v0:
```python
import jax
import jax.numpy as jnp
from jax import lax
from jax.sharding import PartitionSpec as P

HEADS = 32
KV_HEADS = 4
HD = 128
EPSILON = 1e-06


def normalize_layer(values, gain, shift):
    middle = jnp.mean(values, axis=-1, keepdims=True)
    centered = values - middle
    spread = jnp.mean(centered * centered, axis=-1, keepdims=True)
    return centered * lax.rsqrt(spread + EPSILON) * gain + shift


def normalize_heads(values):
    return values * lax.rsqrt(jnp.mean(values * values, axis=-1, keepdims=True) + EPSILON)


def gelu_slope(values):
    return (
        0.5 * (1.0 + lax.erf(values * 0.7071067811865476))
        + values * jnp.exp(-0.5 * values * values) * 0.3989422804014327
    )


def encoder_rows(rows, fc1_weight, fc1_bias, fc2_weight):
    pre = (
        lax.dot_general(
            rows, fc1_weight, (((1,), (1,)), ((), ())), preferred_element_type=jnp.float32
        )
        + fc1_bias
    )
    hidden = jax.nn.gelu(pre, approximate=False).astype(jnp.bfloat16)
    partial_sum = jnp.dot(hidden, fc2_weight, preferred_element_type=jnp.float32)
    return (pre, hidden, partial_sum)


def weight_terms(rows, pre, hidden, cotangent, fc2_weight):
    hidden_grad = lax.dot_general(
        cotangent, fc2_weight, (((1,), (1,)), ((), ())), preferred_element_type=jnp.float32
    )
    second_term = lax.dot_general(
        hidden, cotangent, (((0,), (0,)), ((), ())), preferred_element_type=jnp.float32
    )
    pre_grad = (hidden_grad * gelu_slope(pre)).astype(jnp.bfloat16)
    first_term = lax.dot_general(
        pre_grad, rows, (((0,), (0,)), ((), ())), preferred_element_type=jnp.float32
    )
    return (first_term, second_term)


def project_heads(states, key_columns, value_columns, heads):
    width = states.shape[-1]
    key_raw = jnp.einsum(
        "rd,dhe->hre",
        states,
        key_columns.reshape(width, heads, HD),
        preferred_element_type=jnp.float32,
    )
    keys = normalize_heads(key_raw).astype(jnp.bfloat16)
    values = jnp.einsum(
        "rd,dhe->hre",
        states,
        value_columns.reshape(width, heads, HD),
        preferred_element_type=jnp.float32,
    ).astype(jnp.bfloat16)
    return (keys, values)


def on_device(
    images,
    ln_gain,
    ln_bias,
    fc1_weight,
    fc1_bias,
    fc2_weight,
    fc2_bias,
    key_weight,
    value_weight,
    text,
    query_weight,
    tiles,
    links,
    lengths,
    state_grads,
):
    dec_count = lax.axis_size("dec")
    grp_count = lax.axis_size("grp")
    enc_place = lax.axis_index("enc")
    dec_place = lax.axis_index("dec")
    grp_place = lax.axis_index("grp")
    slots = images.shape[1]
    patch = images.shape[2]
    width = images.shape[3]
    img_rows = slots * patch
    own_rows = images.reshape(img_rows, width)
    normed = normalize_layer(own_rows.astype(jnp.float32), ln_gain, ln_bias).astype(jnp.bfloat16)
    samples = text.shape[0]
    length = text.shape[1]
    text_rows = text.reshape(samples * length, text.shape[2])
    half = query_weight.shape[1] // grp_count
    own_half = lax.dynamic_slice_in_dim(query_weight, grp_place * half, half, 1)
    gathered, half_rows = (
        lax.all_gather(normed, "enc", axis=0, tiled=True),
        lax.all_gather(own_half, "enc", axis=0, tiled=True),
    )
    query_raw = jnp.dot(
        text_rows,
        lax.all_gather(half_rows, "grp", axis=1, tiled=True),
        preferred_element_type=jnp.float32,
    )
    tile_index = jnp.arange(slots)
    pre, hidden, partial_full = encoder_rows(gathered, fc1_weight, fc1_bias, fc2_weight)
    summed = lax.psum_scatter(
        partial_full.astype(jnp.bfloat16), "enc", scatter_dimension=0, tiled=True
    ).astype(jnp.float32)
    states = (own_rows.astype(jnp.float32) + summed + fc2_bias).astype(jnp.bfloat16)
    local_heads = query_weight.shape[1] // HD
    per_group = HEADS // KV_HEADS
    kv_local = max(1, local_heads // per_group)
    first_head = dec_place * local_heads // per_group
    key_columns = lax.dynamic_slice_in_dim(key_weight, first_head * HD, kv_local * HD, 1)
    value_columns = lax.dynamic_slice_in_dim(value_weight, first_head * HD, kv_local * HD, 1)
    piece = lax.all_gather(states.reshape(1, img_rows, width), "dec", axis=0, tiled=True)
    count = piece.shape[0]
    key_part, value_part = project_heads(
        piece.reshape(count * img_rows, width), key_columns, value_columns, kv_local
    )
    key_part = key_part.reshape(kv_local, count, img_rows, HD).transpose(1, 0, 2, 3)
    value_part = value_part.reshape(kv_local, count, img_rows, HD).transpose(1, 0, 2, 3)
    paired = jnp.stack([key_part, value_part])
    keys = paired[0]
    values = paired[1]
    heads_each = local_heads // kv_local
    queries = normalize_heads(query_raw.reshape(samples, length, local_heads, HD)).astype(
        jnp.bfloat16
    )
    queries = queries.reshape(samples, length, kv_local, heads_each, HD)
    dec_tiles = tiles[enc_place, :, grp_place]
    live_keys = tile_index[None, :] < dec_tiles[:, None]
    live_keys = jnp.broadcast_to(live_keys[:, :, None], (dec_count, slots, patch)).reshape(
        dec_count, img_rows
    )
    allowed = (links[:, :, None] > 0) & live_keys[None, :, :]
    scores = jnp.einsum(
        "sqghd,jgkd->sghjkq", queries, keys, preferred_element_type=jnp.float32
    ) * HD ** (-0.5)
    weights = jnp.where(allowed[:, None, None, :, :, None], jnp.exp(scores), 0.0)
    totals = jnp.sum(weights, axis=(3, 4), keepdims=True)
    probs = (weights / totals).astype(jnp.bfloat16)
    mixed = jnp.einsum("sghjkq,jgkd->sqghd", probs, values, preferred_element_type=jnp.float32)
    valid = jnp.arange(length)[None, :] < lengths[:, None]
    context = (
        jnp.where(valid[:, :, None, None, None], mixed, 0.0)
        .reshape(samples, length, local_heads * HD)
        .astype(jnp.bfloat16)
    )
    own_tiles = tiles[enc_place, dec_place, grp_place]
    own_live = jnp.broadcast_to((tile_index < own_tiles)[:, None, None], (slots, patch, 1)).reshape(
        img_rows, 1
    )
    cotangent = jnp.where(
        own_live, state_grads.reshape(img_rows, width), jnp.zeros((), state_grads.dtype)
    )
    all_cotangent = lax.all_gather(cotangent, "enc", axis=0, tiled=True)
    first_term, second_term = weight_terms(gathered, pre, hidden, all_cotangent, fc2_weight)
    fc1_grad, fc2_grad = (
        lax.psum_scatter(
            first_term.astype(jnp.bfloat16), ("dec", "grp"), scatter_dimension=0, tiled=True
        ).astype(jnp.float32),
        lax.psum_scatter(
            second_term.astype(jnp.bfloat16), ("dec", "grp"), scatter_dimension=0, tiled=True
        ).astype(jnp.float32),
    )
    return (context, fc1_grad, fc2_grad)


def solution(mesh):
    in_specs = (
        P(("enc", "dec", "grp"), None, None, None),
        P(),
        P(),
        P("enc", None),
        P("enc"),
        P("enc", None),
        P(),
        P(),
        P(),
        P(("enc", "grp"), None, None),
        P("enc", "dec"),
        P(),
        P(("enc", "grp"), None),
        P(("enc", "grp")),
        P(("enc", "dec", "grp"), None, None, None),
    )
    out_specs = (
        P(("enc", "grp"), None, "dec"),
        P(("enc", "dec", "grp"), None),
        P(("enc", "dec", "grp"), None),
    )
    return jax.shard_map(
        on_device, mesh=mesh, in_specs=in_specs, out_specs=out_specs, check_vma=False
    )
```

profile of v0, /device:TPU:0, one launch (start us, length us, event | category | flops | bytes accessed | tf_op | source)
XLA Modules:
  0.0 579.2 jit_solution(997100307381949104)
XLA Ops:
  7.2 1.2 convert_reduce_fusion
  8.4 0.1 div.40
  8.5 1.2 fusion.29
  9.8 0.1 rsqrt.31
  9.8 2.0 fusion.33
  11.9 1.3 dynamic_slice.19
  13.2 0.6 iota_compare_fusion.2
  13.8 0.1 broadcast_in_dim.70
  13.9 0.1 broadcast_in_dim.71
  14.0 1.8 bitcast_select_fusion.2
  15.9 3.3 constant_dynamic-slice_fusion
  19.2 49.9 %all-gather.6.cloned.1.call-done = bf16[1024,1280]{1,0:T(8,128)(2,1)} async-done(((bf16[128,1280]{1,0:T(8,128)(2,1)}), bf16[1024,1280]{1,0:T(8,128)(2,1)}) %all-gather.6.cloned.1.call-update) | async-done | bytes 2621456 | tf_op jit(solution)/shard_map/all_gather | solution.py:108
  69.1 10.1 %fusion.3 = (bf16[1024,640]{1,0:T(8,128)(2,1)}, f32[1024,640]{1,0:T(8,128)}) fusion(f32[640]{0:T(1024)S(1)} %copy-done.6, bf16[1024,1280]{1,0:T(8,128)(2,1)} %all-gather.6.cloned.1.call-done, bf16[640,1280]{1,0:T(8,128)(2,1)S(1)} %copy-done.5), kind=kOutput, calls=%fused_computation.11 | convolution fusion | flops 1720975360 | bytes 8194560 | tf_op jit(solution)/shard_map/dot_general | solution.py:32
  79.2 45.7 %all-gather.12.cloned.1.call-done = bf16[1024,1280]{1,0:T(8,128)(2,1)} async-done(((bf16[128,1280]{1,0:T(8,128)(2,1)}), bf16[1024,1280]{1,0:T(8,128)(2,1)}) %all-gather.12.cloned.1.call-update) | async-done | bytes 2621456 | tf_op jit(solution)/shard_map/all_gather | solution.py:169
  124.9 11.8 %convolution_convert_fusion.2 = bf16[640,1280]{1,0:T(8,128)(2,1)} fusion(bf16[1024,1280]{1,0:T(8,128)(2,1)} %all-gather.6.cloned.1.call-done, f32[1024,640]{1,0:T(8,128)} %get-tuple-element.13, bf16[1024,1280]{1,0:T(8,128)(2,1)} %all-gather.12.cloned.1.call-done, bf16[640,1280]{1,0:T(8,128)(2,1)S(1)} %copy-done, f32[640]{0:T(1024)S(1)} %copy-done.6), kind=kOutput, calls=%fused_computation.7 | convolution fusion | flops 3363471360 | bytes 11143680 | tf_op jit(solution)/shard_map/dot_general | solution.py:50
  136.7 5.2 convolution_convert_fusion.1
  142.0 0.2 reduce-scatter.4.cloned.1.call-start
  142.2 3.7 convolution_convert_fusion
  146.0 206.9 %all-gather.8.cloned.1.call-done = bf16[8192,1024]{1,0:T(8,128)(2,1)} async-done(((bf16[1024,1024]{1,0:T(8,128)(2,1)}), bf16[8192,1024]{1,0:T(8,128)(2,1)}) %all-gather.8.cloned.1.call-update) | async-done | bytes 16777232 | tf_op jit(solution)/shard_map/all_gather | solution.py:109
  353.0 0.6 copy-done.7
  353.6 0.1 copy.48
  353.7 0.2 dynamic-slice_reduce_fusion
  353.9 0.1 iota_compare_fusion
  354.0 0.1 broadcast_in_dim.39
  354.1 0.1 and.29
  354.1 1.4 constant_dynamic-slice_fusion.1
  355.6 0.2 copy.49
  355.8 0.2 copy.46
  356.1 0.1 broadcast_and_fusion
  356.2 25.8 %reduce-scatter.6.cloned.1.call-done = bf16[160,1280]{1,0:T(8,128)(2,1)} async-done(((bf16[640,1280]{1,0:T(8,128)(2,1)}), bf16[160,1280]{1,0:T(8,128)(2,1)}) %reduce-scatter.6.cloned.1.call-update) | async-done | bytes 409616 | tf_op jit(solution)/shard_map/reduce_scatter | solution.py:172
  382.0 1.9 convert_element_type.88
  384.0 28.9 %reduce-scatter.8.cloned.1.call-done = bf16[160,1280]{1,0:T(8,128)(2,1)} async-done(((bf16[640,1280]{1,0:T(8,128)(2,1)}), bf16[160,1280]{1,0:T(8,128)(2,1)}) %reduce-scatter.8.cloned.1.call-update) | async-done | bytes 409616 | tf_op jit(solution)/shard_map/reduce_scatter | solution.py:175
  412.8 1.9 convert_element_type.90
  414.8 72.4 %reduce-scatter.4.cloned.1.call-done = bf16[128,1280]{1,0:T(8,128)(2,1)} async-done(((bf16[1024,1280]{1,0:T(8,128)(2,1)}), bf16[128,1280]{1,0:T(8,128)(2,1)}) %reduce-scatter.4.cloned.1.call-update) | async-done | bytes 327696 | tf_op jit(solution)/shard_map/reduce_scatter | solution.py:118
  487.2 1.1 fusion.35
  488.3 8.7 %all-gather = bf16[256,1280]{1,0:T(8,128)(2,1)S(1)} all-gather(bf16[128,1280]{1,0:T(8,128)(2,1)S(1)} %fusion.35), channel_id=2, replica_groups=mesh['enc'=8,'dec'=2,'grp'=2] {'dec'}, dimensions={0}, use_global_device_ids=true | all-gather | bytes 983040 | tf_op jit(solution)/shard_map/all_gather | solution.py:128
  497.0 0.4 multiply_reduce_fusion
  497.4 0.1 copy.61
  497.5 0.4 fusion.20
  497.9 41.0 %all-gather.10.cloned.1.call-done = bf16[8192,2048]{1,0:T(8,128)(2,1)} async-done(((bf16[8192,1024]{1,0:T(8,128)(2,1)}), bf16[8192,2048]{1,0:T(8,128)(2,1)}) %all-gather.10.cloned.1.call-update) | async-done | bytes 33554448 | tf_op jit(solution)/shard_map/all_gather | solution.py:113
  538.9 17.7 %fusion.48 = (f32[256,2048]{0,1:T(8,128)}, f32[256,2048]{0,1:T(8,128)}) fusion(bf16[8192,2048]{1,0:T(8,128)(2,1)} %all-gather.10.cloned.1.call-done, bf16[256,8192]{1,0:T(8,128)(2,1)} %bitcast.111), kind=kOutput, calls=%fused_computation.87 | convolution fusion | flops 8590458880 | bytes 41943040 | tf_op jit(solution)/shard_map/dot_general | solution.py:111
  556.6 2.3 mul.116
  558.9 3.3 reshape.170
  562.2 4.1 copy.53
  566.3 0.6 reduce_sum.48
  566.9 2.9 fusion
  569.8 1.2 fusion.19
  571.1 1.3 copy.56
  (39 shorter events, 0.6 us)
Async XLA Ops:
  7.2 117.7 %copy-start = (bf16[640,1280]{1,0:T(8,128)(2,1)S(1)}, bf16[640,1280]{1,0:T(8,128)(2,1)}, u32[]{:S(2)}) copy-start(bf16[640,1280]{1,0:T(8,128)(2,1)} %param.20) | copy-start | bytes 4915204
  7.2 61.9 %all-gather.6.cloned.1.call-start = ((), (), s32[]{:S(2)}) async-start(), calls=%async_computation.3 | async-start | bytes 2949120 | tf_op jit(solution)/shard_map/all_gather | solution.py:108
  11.8 113.0 %all-gather.12.cloned.1.call-start = ((), (), s32[]{:S(2)}) async-start(), calls=%async_computation.7 | async-start | bytes 2949120 | tf_op jit(solution)/shard_map/all_gather | solution.py:169
  15.8 337.1 %all-gather.8.cloned.1.call-start = ((), (), s32[]{:S(2)}) async-start(), calls=%async_computation.5 | async-start | bytes 18874368 | tf_op jit(solution)/shard_map/all_gather | solution.py:109
  15.9 53.3 %copy-start.5 = (bf16[640,1280]{1,0:T(8,128)(2,1)S(1)}, bf16[640,1280]{1,0:T(8,128)(2,1)}, u32[]{:S(2)}) copy-start(bf16[640,1280]{1,0:T(8,128)(2,1)} %param.18) | copy-start | bytes 4915204
  15.9 53.3 %copy-start.6 = (f32[640]{0:T(1024)S(1)}, f32[640]{0:T(1024)}, u32[]{:S(2)}) copy-start(f32[640]{0:T(1024)} %param.19) | copy-start | bytes 7684
  19.2 362.8 %reduce-scatter.6.cloned.1.call-start = ((), (), s32[]{:S(2)}) async-start(), calls=%async_computation.8 | async-start | bytes 2048000 | tf_op jit(solution)/shard_map/reduce_scatter | solution.py:172
  124.9 11.8 %copy-start.9 = (bf16[1024,640]{1,0:T(8,128)(2,1)S(1)}, bf16[1024,640]{1,0:T(8,128)(2,1)}, u32[]{:S(2)}) copy-start(bf16[1024,640]{1,0:T(8,128)(2,1)} %get-tuple-element.12) | copy-start | bytes 3932164
  136.7 276.2 %reduce-scatter.8.cloned.1.call-start = ((), (), s32[]{:S(2)}) async-start(), calls=%async_computation.9 | async-start | bytes 2048000 | tf_op jit(solution)/shard_map/reduce_scatter | solution.py:175
  142.0 345.2 %reduce-scatter.4.cloned.1.call-start = ((), (), s32[]{:S(2)}) async-start(), calls=%async_computation.4 | async-start | bytes 2949120 | tf_op jit(solution)/shard_map/reduce_scatter | solution.py:118
  145.9 393.0 %all-gather.10.cloned.1.call-start = ((), (), s32[]{:S(2)}) async-start(), calls=%async_computation.6 | async-start | bytes 50331648 | tf_op jit(solution)/shard_map/all_gather | solution.py:113
  352.9 0.7 copy-start.7
  352.9 0.8 copy-start.4
  354.1 1.9 copy-start.8
  355.5 131.6 %copy-start.2 = (bf16[1,4,32,1280]{3,2,1,0:T(8,128)(2,1)S(1)}, bf16[1,4,32,1280]{3,2,1,0:T(8,128)(2,1)}, u32[]{:S(2)}) copy-start(bf16[1,4,32,1280]{3,2,1,0:T(8,128)(2,1)} %param.15) | copy-start | bytes 983044
  355.6 131.6 %copy-start.3 = (f32[1280]{0:T(1024)S(1)}, f32[1280]{0:T(1024)}, u32[]{:S(2)}) copy-start(f32[1280]{0:T(1024)} %param.21) | copy-start | bytes 15364
  569.8 2.6 copy-start.1
Sparse Core Ops, SparseCore 0:
  12.0 57.1 all-gather.5
  71.9 52.9 all-gather.11
  127.0 225.8 all-gather.7
  355.3 26.6 reduce-scatter.5
  384.4 28.3 reduce-scatter.7
  416.2 70.9 reduce-scatter.3
  488.7 50.1 all-gather.9
where the time goes:
time: 580 us; the launch traced here: 579 us
  waiting for transfers between devices  471 us (81%)
  matrix products  53.3 us (9%)
  local copies, waits for them, and re-layouts  19.1 us (3%)
  between operations  14.3 us (2%)
  other arithmetic  12.6 us (2%)
  blocking collectives  8.7 us (1%)
    all_gather x1, waiting for transfers between devices, on_device(): lax.all_gather(own_half, 'enc', axis=0, tiled=True)  207 us
    reduce_scatter x1, waiting for transfers between devices, on_device(): lax.psum_scatter(partial_full.astype(jnp.bfloat16), 'enc', scatter_dimens...  72.4 us
    all_gather x1, waiting for transfers between devices, on_device(): lax.all_gather(normed, 'enc', axis=0, tiled=True)  49.9 us
    all_gather x1, waiting for transfers between devices, on_device(): all_cotangent = lax.all_gather(cotangent, 'enc', axis=0, tiled=True)  45.7 us
    all_gather x1, waiting for transfers between devices, on_device(): lax.all_gather(half_rows, 'grp', axis=1, tiled=True)  41 us
    reduce_scatter x1, waiting for transfers between devices, on_device(): lax.psum_scatter(second_term.astype(jnp.bfloat16), ('dec', 'grp'), scatte...  28.9 us
    reduce_scatter x1, waiting for transfers between devices, on_device(): lax.psum_scatter(first_term.astype(jnp.bfloat16), ('dec', 'grp'), scatter...  25.8 us
    dot_general x1, matrix products, on_device(): jnp.dot(text_rows, lax.all_gather(half_rows, 'grp', axis=1, tiled=True),...  17.7 us
  transfers between devices with their start and end apart: 7, of which 7 were waited for; matrix products, arithmetic and copies ran while one was open for 8% of the time, Pallas kernels for 0%

commit v1 on v0

--- a/solution.py
+++ b/solution.py
@@ -166,7 +166,21 @@
     cotangent = jnp.where(
         own_live, state_grads.reshape(img_rows, width), jnp.zeros((), state_grads.dtype)
     )
-    all_cotangent = lax.all_gather(cotangent, "enc", axis=0, tiled=True)
+
+    def compute_the_widths(block_in, dim_no):
+        chip_axis = "enc"
+        n_dev_all = lax.axis_size(chip_axis)
+        q_next = sorted(((to_i, (to_i + 1) % n_dev_all) for to_i in range(n_dev_all)))
+        low = block_in
+        sheets = [low]
+        for q in range(1, n_dev_all):
+            low = lax.ppermute(low, chip_axis, q_next)
+            sheets.insert(0, low)
+        prior = jnp.concatenate(sheets, axis=dim_no)
+        found_now = lax.axis_index(chip_axis) + 1
+        return jnp.roll(prior, found_now * block_in.shape[dim_no], axis=dim_no)
+
+    all_cotangent = compute_the_widths(cotangent, 0)
     first_term, second_term = weight_terms(gathered, pre, hidden, all_cotangent, fc2_weight)
     fc1_grad, fc2_grad = (
         lax.psum_scatter(

time: 580 us -> 551 us (0.950)
  waiting for transfers between devices: 471 us -> 425 us
  local copies, waits for them, and re-layouts: 19.1 us -> 35 us
    ppermute x0 -> x7, waiting for transfers between devices: none -> 111 us  [compute_the_widths(): low = lax.ppermute(low, chip_axis, q_next)]
    all_gather x1, waiting for transfers between devices: 207 us -> 146 us  [on_device(): lax.all_gather(own_half, 'enc', axis=0, tiled=True)]
    all_gather x1, waiting for transfers between devices: 49.9 us -> 0.01 us  [on_device(): lax.all_gather(normed, 'enc', axis=0, tiled=True)]
    all_gather x1 -> x0, waiting for transfers between devices: 45.7 us -> none  [on_device(): all_cotangent = lax.all_gather(cotangent, 'enc', axis=0, tiled=True)]
    unnamed x21 -> x36, local copies, waits for them, and re-layouts: 2 us -> 19.7 us
  transfers between devices with their start and end apart: 7 -> 13, of which waited for: 7 -> 12; matrix products, arithmetic and copies ran while one was open for 8% -> 11% of each run, Pallas kernels for 0% -> 0%
where the time goes in v1:
time: 551 us; the launch traced here: 550 us
  waiting for transfers between devices  425 us (77%)
  matrix products  51.3 us (9%)
  local copies, waits for them, and re-layouts  35 us (6%)
  between operations  14.3 us (3%)
  other arithmetic  12.5 us (2%)
  blocking collectives  8.7 us (2%)
    all_gather x1, waiting for transfers between devices, on_device(): lax.all_gather(own_half, 'enc', axis=0, tiled=True)  146 us
    ppermute x7, waiting for transfers between devices, compute_the_widths(): low = lax.ppermute(low, chip_axis, q_next)  111 us
    reduce_scatter x1, waiting for transfers between devices, on_device(): lax.psum_scatter(partial_full.astype(jnp.bfloat16), 'enc', scatter_dimens...  72.5 us
    all_gather x1, waiting for transfers between devices, on_device(): lax.all_gather(half_rows, 'grp', axis=1, tiled=True)  40.9 us
    reduce_scatter x1, waiting for transfers between devices, on_device(): lax.psum_scatter(second_term.astype(jnp.bfloat16), ('dec', 'grp'), scatte...  28.9 us
    reduce_scatter x1, waiting for transfers between devices, on_device(): lax.psum_scatter(first_term.astype(jnp.bfloat16), ('dec', 'grp'), scatter...  25.5 us
    unnamed x36, local copies, waits for them, and re-layouts  19.7 us
    dot_general x1, matrix products, on_device(): jnp.dot(text_rows, lax.all_gather(half_rows, 'grp', axis=1, tiled=True),...  17.3 us
  transfers between devices with their start and end apart: 13, of which 12 were waited for; matrix products, arithmetic and copies ran while one was open for 11% of the time, Pallas kernels for 0%

profile of v1, /device:TPU:0, one launch (start us, length us, event | category | flops | bytes accessed | tf_op | source)
XLA Modules:
  0.0 550.2 jit_solution(2436843301166025568)
XLA Ops:
  7.2 1.2 convert_reduce_fusion
  8.4 1.2 fusion.36
  9.8 2.0 fusion.40
  11.9 3.1 constant_dynamic-slice_fusion
  16.7 3.0 collective-permute-start
  19.7 13.7 %collective-permute-done = bf16[128,1280]{1,0:T(8,128)(2,1)S(1)} collective-permute-done((bf16[128,1280]{1,0:T(8,128)(2,1)S(1)}, bf16[128,1280]{1,0:T(8,128)(2,1)S(1)}, u32[]{:S(2)}, u32[]{:S(2)}) %collective-permute-start) | collective-permute-done | bytes 327712 | tf_op jit(solution)/shard_map/ppermute | solution.py:177
  33.4 14.6 %collective-permute-done.1 = bf16[128,1280]{1,0:T(8,128)(2,1)S(1)} collective-permute-done((bf16[128,1280]{1,0:T(8,128)(2,1)S(1)}, bf16[128,1280]{1,0:T(8,128)(2,1)S(1)}, u32[]{:S(2)}, u32[]{:S(2)}) %collective-permute-start.1) | collective-permute-done | bytes 327712 | tf_op jit(solution)/shard_map/ppermute | solution.py:177
  48.1 19.1 %collective-permute-done.2 = bf16[128,1280]{1,0:T(8,128)(2,1)S(1)} collective-permute-done((bf16[128,1280]{1,0:T(8,128)(2,1)S(1)}, bf16[128,1280]{1,0:T(8,128)(2,1)S(1)}, u32[]{:S(2)}, u32[]{:S(2)}) %collective-permute-start.2) | collective-permute-done | bytes 327712 | tf_op jit(solution)/shard_map/ppermute | solution.py:177
  67.2 19.0 %collective-permute-done.3 = bf16[128,1280]{1,0:T(8,128)(2,1)S(1)} collective-permute-done((bf16[128,1280]{1,0:T(8,128)(2,1)S(1)}, bf16[128,1280]{1,0:T(8,128)(2,1)S(1)}, u32[]{:S(2)}, u32[]{:S(2)}) %collective-permute-start.3) | collective-permute-done | bytes 327712 | tf_op jit(solution)/shard_map/ppermute | solution.py:177
  86.2 9.9 %collective-permute-done.4 = bf16[128,1280]{1,0:T(8,128)(2,1)} collective-permute-done((bf16[128,1280]{1,0:T(8,128)(2,1)S(1)}, bf16[128,1280]{1,0:T(8,128)(2,1)}, u32[]{:S(2)}, u32[]{:S(2)}) %collective-permute-start.4) | collective-permute-done | bytes 327712 | tf_op jit(solution)/shard_map/ppermute | solution.py:177
  96.1 17.0 %collective-permute-done.5 = bf16[128,1280]{1,0:T(8,128)(2,1)} collective-permute-done((bf16[128,1280]{1,0:T(8,128)(2,1)}, bf16[128,1280]{1,0:T(8,128)(2,1)}, u32[]{:S(2)}, u32[]{:S(2)}) %collective-permute-start.5) | collective-permute-done | bytes 327712 | tf_op jit(solution)/shard_map/ppermute | solution.py:177
  113.1 17.2 %collective-permute-done.6 = bf16[128,1280]{1,0:T(8,128)(2,1)} collective-permute-done((bf16[128,1280]{1,0:T(8,128)(2,1)}, bf16[128,1280]{1,0:T(8,128)(2,1)}, u32[]{:S(2)}, u32[]{:S(2)}) %collective-permute-start.6) | collective-permute-done | bytes 327712 | tf_op jit(solution)/shard_map/ppermute | solution.py:177
  130.3 1.7 constant_dynamic-update-slice_fusion.15
  132.0 1.7 constant_dynamic-update-slice_fusion.14
  133.7 1.7 constant_dynamic-update-slice_fusion.13
  135.4 0.8 constant_dynamic-update-slice_fusion.12
  136.2 0.7 constant_dynamic-update-slice_fusion.11
  136.9 0.7 constant_dynamic-update-slice_fusion.10
  139.2 1.8 constant_dynamic-update-slice_fusion.7
  140.9 1.7 constant_dynamic-update-slice_fusion.6
  142.6 1.7 constant_dynamic-update-slice_fusion.5
  144.4 0.8 constant_dynamic-update-slice_fusion.4
  145.9 0.8 constant_dynamic-update-slice_fusion.2
  146.6 0.8 constant_dynamic-update-slice_fusion.1
  147.4 0.7 constant_dynamic-update-slice_fusion
  148.1 10.4 %fusion.3 = (bf16[1024,640]{1,0:T(8,128)(2,1)S(1)}, f32[1024,640]{1,0:T(8,128)}) fusion(f32[640]{0:T(1024)S(1)} %copy-done.7, bf16[1024,1280]{1,0:T(8,128)(2,1)} %all-gather.5.cloned.1.call-done, bf16[640,1280]{1,0:T(8,128)(2,1)} %param.18), kind=kOutput, calls=%fused_computation.11 | convolution fusion | flops 1720975360 | bytes 8194560 | tf_op jit(solution)/shard_map/dot_general | solution.py:32
  158.5 11.7 %convolution_convert_fusion.2 = bf16[640,1280]{1,0:T(8,128)(2,1)} fusion(bf16[1024,1280]{1,0:T(8,128)(2,1)} %all-gather.5.cloned.1.call-done, f32[1024,640]{1,0:T(8,128)} %get-tuple-element.13, bf16[640,1280]{1,0:T(8,128)(2,1)S(1)} %copy-done, bf16[2048,1280]{1,0:T(8,128)(2,1)} %constant_dynamic-update-slice_fusion, s32[]{:T(128)S(6)} %select_n.58, ...), kind=kOutput, calls=%fused_computation.7 | convolution fusion | flops 3363471360 | bytes 11143684 | tf_op jit(solution)/shard_map/dot_general | solution.py:50
  170.4 4.8 convolution_convert_fusion.1
  175.3 3.7 convolution_convert_fusion
  179.1 146.5 %all-gather.7.cloned.1.call-done = bf16[8192,1024]{1,0:T(8,128)(2,1)} async-done(((bf16[1024,1024]{1,0:T(8,128)(2,1)}), bf16[8192,1024]{1,0:T(8,128)(2,1)}) %all-gather.7.cloned.1.call-update) | async-done | bytes 16777232 | tf_op jit(solution)/shard_map/all_gather | solution.py:109
  325.6 1.3 copy-done.4
  326.9 1.2 constant_dynamic-slice_fusion.1
  329.3 25.5 %reduce-scatter.6.cloned.1.call-done = bf16[160,1280]{1,0:T(8,128)(2,1)} async-done(((bf16[640,1280]{1,0:T(8,128)(2,1)}), bf16[160,1280]{1,0:T(8,128)(2,1)}) %reduce-scatter.6.cloned.1.call-update) | async-done | bytes 409616 | tf_op jit(solution)/shard_map/reduce_scatter | solution.py:186
  354.8 1.9 convert_element_type.88
  356.7 28.9 %reduce-scatter.8.cloned.1.call-done = bf16[160,1280]{1,0:T(8,128)(2,1)} async-done(((bf16[640,1280]{1,0:T(8,128)(2,1)}), bf16[160,1280]{1,0:T(8,128)(2,1)}) %reduce-scatter.8.cloned.1.call-update) | async-done | bytes 409616 | tf_op jit(solution)/shard_map/reduce_scatter | solution.py:189
  385.6 1.9 convert_element_type.90
  387.6 72.5 %reduce-scatter.4.cloned.1.call-done = bf16[128,1280]{1,0:T(8,128)(2,1)} async-done(((bf16[1024,1280]{1,0:T(8,128)(2,1)}), bf16[128,1280]{1,0:T(8,128)(2,1)}) %reduce-scatter.4.cloned.1.call-update) | async-done | bytes 327696 | tf_op jit(solution)/shard_map/reduce_scatter | solution.py:118
  460.1 1.1 fusion.42
  461.2 8.7 %all-gather = bf16[256,1280]{1,0:T(8,128)(2,1)S(1)} all-gather(bf16[128,1280]{1,0:T(8,128)(2,1)S(1)} %fusion.42), channel_id=2, replica_groups=mesh['enc'=8,'dec'=2,'grp'=2] {'dec'}, dimensions={0}, use_global_device_ids=true | all-gather | bytes 983040 | tf_op jit(solution)/shard_map/all_gather | solution.py:128
  470.8 40.9 %all-gather.9.cloned.1.call-done = bf16[8192,2048]{1,0:T(8,128)(2,1)} async-done(((bf16[8192,1024]{1,0:T(8,128)(2,1)}), bf16[8192,2048]{1,0:T(8,128)(2,1)}) %all-gather.9.cloned.1.call-update) | async-done | bytes 33554448 | tf_op jit(solution)/shard_map/all_gather | solution.py:113
  511.6 17.3 %fusion.59 = (f32[256,2048]{0,1:T(8,128)}, f32[256,2048]{0,1:T(8,128)S(1)}) fusion(bf16[8192,2048]{1,0:T(8,128)(2,1)} %all-gather.9.cloned.1.call-done, bf16[256,8192]{1,0:T(8,128)(2,1)} %bitcast.109), kind=kOutput, calls=%fused_computation.109 | convolution fusion | flops 8590458880 | bytes 41943040 | tf_op jit(solution)/shard_map/dot_general | solution.py:111
  528.9 2.1 reshape.170
  531.0 2.8 copy.53
  533.8 3.3 mul.119
  537.1 2.1 reduce_sum.48
  539.2 1.5 fusion
  540.8 1.2 fusion.24
  542.1 1.3 copy.56
  (66 shorter events, 6.6 us)
Async XLA Ops:
  7.2 151.3 %copy-start = (bf16[640,1280]{1,0:T(8,128)(2,1)S(1)}, bf16[640,1280]{1,0:T(8,128)(2,1)}, u32[]{:S(2)}) copy-start(bf16[640,1280]{1,0:T(8,128)(2,1)} %param.20) | copy-start | bytes 4915204
  7.2 140.9 %all-gather.5.cloned.1.call-start = ((), (), s32[]{:S(2)}) async-start(), calls=%async_computation.3 | async-start | bytes 2949120 | tf_op jit(solution)/shard_map/all_gather | solution.py:108
  11.8 313.7 %all-gather.7.cloned.1.call-start = ((), (), s32[]{:S(2)}) async-start(), calls=%async_computation.5 | async-start | bytes 18874368 | tf_op jit(solution)/shard_map/all_gather | solution.py:109
  11.9 3.3 copy-start.6
  11.9 4.7 copy-start.3
  15.1 339.7 %reduce-scatter.6.cloned.1.call-start = ((), (), s32[]{:S(2)}) async-start(), calls=%async_computation.7 | async-start | bytes 2048000 | tf_op jit(solution)/shard_map/reduce_scatter | solution.py:186
  16.7 16.7 %collective-permute-start = (bf16[128,1280]{1,0:T(8,128)(2,1)S(1)}, bf16[128,1280]{1,0:T(8,128)(2,1)S(1)}, u32[]{:S(2)}, u32[]{:S(2)}) collective-permute-start(bf16[128,1280]{1,0:T(8,128)(2,1)S(1)} %bitcast_select_fusion.2), channel_id=1, source_target_pairs={{0,4},{4,8},{8,12},{12,16},{16,20},{20,24},{24,28},{28,0},{1,5},{5... | collective-permute-start | bytes 983048 | tf_op jit(solution)/shard_map/ppermute | solution.py:177
  33.4 14.6 %collective-permute-start.1 = (bf16[128,1280]{1,0:T(8,128)(2,1)S(1)}, bf16[128,1280]{1,0:T(8,128)(2,1)S(1)}, u32[]{:S(2)}, u32[]{:S(2)}) collective-permute-start(bf16[128,1280]{1,0:T(8,128)(2,1)S(1)} %collective-permute-done), channel_id=1, source_target_pairs={{0,4},{4,8},{8,12},{12,16},{16,20},{20,24},{24,28},{28,0},{1,5},{5... | collective-permute-start | bytes 983048 | tf_op jit(solution)/shard_map/ppermute | solution.py:177
  48.0 19.1 %collective-permute-start.2 = (bf16[128,1280]{1,0:T(8,128)(2,1)S(1)}, bf16[128,1280]{1,0:T(8,128)(2,1)S(1)}, u32[]{:S(2)}, u32[]{:S(2)}) collective-permute-start(bf16[128,1280]{1,0:T(8,128)(2,1)S(1)} %collective-permute-done.1), channel_id=1, source_target_pairs={{0,4},{4,8},{8,12},{12,16},{16,20},{20,24},{24,28},{28,0},{1,5},{5... | collective-permute-start | bytes 983048 | tf_op jit(solution)/shard_map/ppermute | solution.py:177
  67.2 19.0 %collective-permute-start.3 = (bf16[128,1280]{1,0:T(8,128)(2,1)S(1)}, bf16[128,1280]{1,0:T(8,128)(2,1)S(1)}, u32[]{:S(2)}, u32[]{:S(2)}) collective-permute-start(bf16[128,1280]{1,0:T(8,128)(2,1)S(1)} %collective-permute-done.2), channel_id=1, source_target_pairs={{0,4},{4,8},{8,12},{12,16},{16,20},{20,24},{24,28},{28,0},{1,5},{5... | collective-permute-start | bytes 983048 | tf_op jit(solution)/shard_map/ppermute | solution.py:177
  86.2 9.9 %collective-permute-start.4 = (bf16[128,1280]{1,0:T(8,128)(2,1)S(1)}, bf16[128,1280]{1,0:T(8,128)(2,1)}, u32[]{:S(2)}, u32[]{:S(2)}) collective-permute-start(bf16[128,1280]{1,0:T(8,128)(2,1)S(1)} %collective-permute-done.3), channel_id=1, source_target_pairs={{0,4},{4,8},{8,12},{12,16},{16,20},{20,24},{24,28},{28,0},{1,5},{5... | collective-permute-start | bytes 983048 | tf_op jit(solution)/shard_map/ppermute | solution.py:177
  96.1 17.0 %collective-permute-start.5 = (bf16[128,1280]{1,0:T(8,128)(2,1)}, bf16[128,1280]{1,0:T(8,128)(2,1)}, u32[]{:S(2)}, u32[]{:S(2)}) collective-permute-start(bf16[128,1280]{1,0:T(8,128)(2,1)} %collective-permute-done.4), channel_id=1, source_target_pairs={{0,4},{4,8},{8,12},{12,16},{16,20},{20,24},{24,28},{28,0},{1,5},{5... | collective-permute-start | bytes 983048 | tf_op jit(solution)/shard_map/ppermute | solution.py:177
  113.1 17.2 %collective-permute-start.6 = (bf16[128,1280]{1,0:T(8,128)(2,1)}, bf16[128,1280]{1,0:T(8,128)(2,1)}, u32[]{:S(2)}, u32[]{:S(2)}) collective-permute-start(bf16[128,1280]{1,0:T(8,128)(2,1)} %collective-permute-done.5), channel_id=1, source_target_pairs={{0,4},{4,8},{8,12},{12,16},{16,20},{20,24},{24,28},{28,0},{1,5},{5... | collective-permute-start | bytes 983048 | tf_op jit(solution)/shard_map/ppermute | solution.py:177
  139.2 9.0 %copy-start.7 = (f32[640]{0:T(1024)S(1)}, f32[640]{0:T(1024)}, u32[]{:S(2)}) copy-start(f32[640]{0:T(1024)} %param.19) | copy-start | bytes 7684
  170.2 215.4 %reduce-scatter.8.cloned.1.call-start = ((), (), s32[]{:S(2)}) async-start(), calls=%async_computation.8 | async-start | bytes 2048000 | tf_op jit(solution)/shard_map/reduce_scatter | solution.py:189
  175.3 284.8 %reduce-scatter.4.cloned.1.call-start = ((), (), s32[]{:S(2)}) async-start(), calls=%async_computation.4 | async-start | bytes 2949120 | tf_op jit(solution)/shard_map/reduce_scatter | solution.py:118
  179.0 332.6 %all-gather.9.cloned.1.call-start = ((), (), s32[]{:S(2)}) async-start(), calls=%async_computation.6 | async-start | bytes 50331648 | tf_op jit(solution)/shard_map/all_gather | solution.py:113
  325.5 1.3 copy-start.4
  325.6 3.2 copy-start.8
  326.9 2.3 copy-start.9
  328.1 132.0 %copy-start.2 = (bf16[1,4,32,1280]{3,2,1,0:T(8,128)(2,1)S(1)}, bf16[1,4,32,1280]{3,2,1,0:T(8,128)(2,1)}, u32[]{:S(2)}) copy-start(bf16[1,4,32,1280]{3,2,1,0:T(8,128)(2,1)} %param.15) | copy-start | bytes 983044
  328.1 132.0 %copy-start.5 = (f32[1280]{0:T(1024)S(1)}, f32[1280]{0:T(1024)}, u32[]{:S(2)}) copy-start(f32[1280]{0:T(1024)} %param.21) | copy-start | bytes 15364
  540.8 2.6 copy-start.1
Sparse Core Ops, SparseCore 0:
  12.0 72.1 all-gather.4
  86.3 239.2 all-gather.6
  328.1 26.6 reduce-scatter.5
  357.2 28.3 reduce-scatter.7
  389.0 71.0 reduce-scatter.3
  461.5 50.1 all-gather.8
